TPU v7x, 32 devices: a whole 2x2x4 slice. The times are simulated.
32 devices in a mesh: tx: 8 (over z, y), ty: 2 (over x), mem: 2 (over core).
Axes of the slice: x: 2, y: 2, z: 4, core: 2. Of those that a mesh axis runs over, the one named last changes fastest.
Arguments:
- obs_value: float32 [262144], P(('tx', 'ty', 'mem')), may hold values from -6 to 6
- obs_frac: float32 [2, 262144], P(None, ('tx', 'ty', 'mem')), may hold values from 0 to 1
- obs_cell: int32 [262144], P(('tx', 'ty', 'mem')), may hold values from 0 to 2047
- obs_layer: int32 [262144], P(('tx', 'ty', 'mem')), may hold values from 0 to 11
- obs_tile: int32 [262144], P(('tx', 'ty', 'mem')), may hold values from 0 to 15, as said below
- obs_length: int32 [32], P(('tx', 'ty', 'mem')), may hold values from 4096 to 8192, as said below
- ensemble: bfloat16 [80, 6, 2, 128, 256], P('mem', None, None, 'tx', 'ty'), may hold values from -6 to 6
Outputs:
- alpha_grad: bfloat16 [80, 2, 128, 256], P('mem', None, 'tx', 'ty')
Inputs may be any that keep to these rules, and one draw needn't show every extreme that they name: `obs_tile`: among the 8192 entries of one device's list, padding included, at most 1536 name one tile; one tile is named by exactly 1536 live entries of every device's list. `obs_length`: every fourth list is full.
All inputs are finite; a program needn't handle non-finite values.
Results may differ from a plain program's by a relative error of at most 0.001.
Values sent between devices are 32-bit elements; how exact they have to be, the bound alone decides.
A program may use at most 64 MiB of HBM per device.

v0:
```python
import math
import jax
import jax.numpy as jnp
from jax import lax
from jax.sharding import PartitionSpec as P


def shifted(block, axis, distance):
    devices = range(lax.axis_size(axis))
    route = [(i - distance, i) for i in devices if i - distance in devices]
    return lax.ppermute(block, axis, route)


def extended_2(x, sides, width):
    for axis, dim in sides:
        size, length = (lax.axis_size(axis), x.shape[dim])
        up = [(i, (i + 1) % size) for i in range(size - 1)]
        down = [(j, i) for i, j in up]
        last = lax.slice_in_dim(x, length - width, length, axis=dim)
        initial = lax.slice_in_dim(x, 0, width, axis=dim)
        before = lax.ppermute(last, axis, up)
        after = lax.ppermute(initial, axis, down)
        x = jnp.concatenate([before, x, after], axis=dim)
    return x


def smooth(padded):
    along_x = 0.25 * padded[:, :, :-2, :] + 0.5 * padded[:, :, 1:-1, :] + 0.25 * padded[:, :, 2:, :]
    return 0.25 * along_x[:, :, :, :-2] + 0.5 * along_x[:, :, :, 1:-1] + 0.25 * along_x[:, :, :, 2:]


def contract_rows(left, right):
    return lax.dot_general(
        left,
        right,
        (((0,), (0,)), ((), ())),
        precision=lax.Precision.HIGHEST,
        preferred_element_type=jnp.float32,
    )


def body(obs_value, obs_frac, obs_cell, obs_layer, obs_tile, obs_length, ensemble):
    tiles_x = lax.axis_size("tx")
    tiles_y = lax.axis_size("ty")
    tile_count = tiles_x * tiles_y
    row_count = obs_value.shape[0]
    capacity = 3 * row_count // tile_count
    slot_count = ensemble.shape[1]
    level_count = ensemble.shape[2]
    cells_x = ensemble.shape[3]
    cells_y = ensemble.shape[4]
    layer_count = slot_count * level_count
    live_rows = jnp.arange(row_count, dtype=jnp.int32) < obs_length[0]
    one_hot = (
        (obs_tile[:, None] == jnp.arange(tile_count, dtype=jnp.int32)[None, :]) & live_rows[:, None]
    ).astype(jnp.float32)
    blocks = one_hot.reshape(row_count // 128, 128, tile_count)
    lower = jnp.arange(128, dtype=jnp.int32)
    triangle = (lower[:, None] >= lower[None, :]).astype(jnp.float32)
    within = jnp.einsum("ij,bjt->bit", triangle, blocks)
    block_totals = jnp.sum(blocks, axis=1)
    offsets = jnp.cumsum(block_totals, axis=0) - block_totals
    ranking = (
        jnp.sum((within + offsets[:, None, :]) * blocks, axis=-1)
        .reshape(row_count)
        .astype(jnp.int32)
        - 1
    )
    position = obs_layer * (cells_x * cells_y) + obs_cell
    payload = jnp.stack([obs_value, obs_frac[0], obs_frac[1], position.astype(jnp.float32)], axis=1)
    send_block = math.gcd(row_count, 2048)
    slot_ids = jnp.arange(capacity, dtype=jnp.int32)

    def place_rows(step, packed):
        start = step * send_block
        hot = lax.dynamic_slice_in_dim(one_hot, start, send_block, 0)
        load = lax.dynamic_slice_in_dim(payload, start, send_block, 0)
        rank = lax.dynamic_slice_in_dim(ranking, start, send_block, 0)
        slots = (rank[:, None] == slot_ids[None, :]).astype(jnp.float32)
        left = (load[:, :, None] * hot[:, None, :]).reshape(send_block, 4 * tile_count)
        return packed + contract_rows(left, slots)

    packed = lax.fori_loop(
        0, row_count // send_block, place_rows, jnp.zeros((4 * tile_count, capacity), jnp.float32)
    )
    packed = packed.reshape(4, tile_count, capacity)
    send_floats = packed[:3]
    send_index = packed[3:4].astype(jnp.int32)
    got_floats, got_index = (
        lax.all_to_all(send_floats, ("tx", "ty"), split_axis=1, concat_axis=1, tiled=True),
        lax.all_to_all(send_index, ("tx", "ty"), split_axis=1, concat_axis=1, tiled=True),
    )
    got_count = tile_count * capacity
    values = got_floats[0].reshape(-1)
    frac_x = got_floats[1].reshape(-1)
    frac_y = got_floats[2].reshape(-1)
    spot = got_index[0].reshape(-1)
    layer = spot // (cells_x * cells_y)
    column = spot % (cells_x * cells_y)
    column_x = column // cells_y
    column_y = column % cells_y
    recv_block = math.gcd(got_count, 2048)
    layer_ids = jnp.arange(layer_count, dtype=jnp.int32)
    xs_ids = jnp.arange(cells_x + 1, dtype=jnp.int32)
    ys_ids = jnp.arange(cells_y, dtype=jnp.int32)

    def spread_rows(step, carry):
        main, rim = carry
        start = step * recv_block
        val = lax.dynamic_slice_in_dim(values, start, recv_block, 0)
        wfx = lax.dynamic_slice_in_dim(frac_x, start, recv_block, 0)
        wfy = lax.dynamic_slice_in_dim(frac_y, start, recv_block, 0)
        lay = lax.dynamic_slice_in_dim(layer, start, recv_block, 0)
        colx = lax.dynamic_slice_in_dim(column_x, start, recv_block, 0)
        coly = lax.dynamic_slice_in_dim(column_y, start, recv_block, 0)
        layer_hot = jnp.where(lay[:, None] == layer_ids[None, :], val[:, None], jnp.float32(0.0))
        weight_x = jnp.where(colx[:, None] == xs_ids[None, :], 1.0 - wfx[:, None], jnp.float32(0.0))
        weight_x = weight_x + jnp.where(
            colx[:, None] + 1 == xs_ids[None, :], wfx[:, None], jnp.float32(0.0)
        )
        weight_y = jnp.where(coly[:, None] == ys_ids[None, :], 1.0 - wfy[:, None], jnp.float32(0.0))
        weight_y = weight_y + jnp.where(
            coly[:, None] + 1 == ys_ids[None, :], wfy[:, None], jnp.float32(0.0)
        )
        rim_weight = jnp.where(coly + 1 == cells_y, wfy, jnp.float32(0.0))
        left = (layer_hot[:, :, None] * weight_x[:, None, :]).reshape(
            recv_block, layer_count * (cells_x + 1)
        )
        main = main + contract_rows(left, weight_y)
        rim = rim + contract_rows(left, rim_weight)
        return (main, rim)

    start_main = jnp.zeros((layer_count * (cells_x + 1), cells_y), jnp.float32)
    start_rim = jnp.zeros((layer_count * (cells_x + 1),), jnp.float32)
    main, rim = lax.fori_loop(0, got_count // recv_block, spread_rows, (start_main, start_rim))
    extended = main.reshape(layer_count, cells_x + 1, cells_y)
    interior = extended[:, :cells_x, :]
    east_rim = extended[:, cells_x, :]
    north_rim = rim.reshape(layer_count, cells_x + 1)
    from_south = shifted(north_rim, "ty", 1)
    interior = interior.at[:, :, 0].add(from_south[:, :cells_x])
    east_rim = east_rim.at[:, 0].add(from_south[:, cells_x])
    from_west = shifted(east_rim, "tx", 1)
    interior = interior.at[:, 0, :].add(from_west)
    grad = lax.psum(interior, "mem")
    grad_slots = grad.reshape(slot_count, level_count, cells_x, cells_y)
    contrib = jnp.sum(ensemble * grad_slots[None], axis=1)
    padded = extended_2(contrib, (("tx", 2), ("ty", 3)), 1)
    return smooth(padded).astype(jnp.bfloat16)


def solution(mesh):
    placed = (
        P(("tx", "ty", "mem")),
        P(None, ("tx", "ty", "mem")),
        P(("tx", "ty", "mem")),
        P(("tx", "ty", "mem")),
        P(("tx", "ty", "mem")),
        P(("tx", "ty", "mem")),
        P("mem", None, None, "tx", "ty"),
    )
    return jax.shard_map(
        body, mesh=mesh, in_specs=placed, out_specs=P("mem", None, "tx", "ty"), check_vma=False
    )
```

profile of v0, /device:TPU:0, one launch (start us, length us, event | category | flops | bytes accessed | tf_op | source)
XLA Modules:
  0.0 210.7 jit_solution(81586102817702164)
XLA Ops:
  11.5 20.3 %while.34 = (s32[]{:T(128)}, f32[64,1536]{1,0:T(8,128)S(1)}, f32[8192,4]{0,1:T(4,128)S(1)}, f32[8192,16]{0,1:T(8,128)S(1)}, s32[8192]{0:T(1024)S(1)}, /*index=5*/s32[]{:T(128)}, s32[]{:T(128)}, s32[]{:T(128)}, s32[]{:T(128)}) while((s32[]{:T(128)}, f32[64,1536]{1,0:T(8,128)S(1)}, f32[8192,4]{0,1:T(4,128)S(1)}, ...), condition=%wide.region_4.5_spmd.clone, body=%wide.region_3.4_spmd.clone.sunk | while | flops 2419392512 | bytes 2351265 | solution.py:83
  11.7 4.9 %fusion.59 = f32[64,1536]{1,0:T(8,128)S(1)} fusion(f32[2048,64]{0,1:T(8,128)S(1)} %bitcast.59, s32[2048]{0:T(1024)S(1)} %dynamic_slice.94, f32[64,1536]{1,0:T(8,128)S(1)} %get-tuple-element.605, pred[]{:T(512)S(6)} %compare.33), kind=kOutput, calls=%fused_computation.7.clone.1 | convolution fusion | flops 2419261440 | bytes 1318913 | tf_op jit(solution)/shard_map/while/body/eval_jaxpr/dot_general | solution.py:33
  16.7 4.9 %fusion.59 = f32[64,1536]{1,0:T(8,128)S(1)} fusion(f32[2048,64]{0,1:T(8,128)S(1)} %bitcast.59, s32[2048]{0:T(1024)S(1)} %dynamic_slice.94, f32[64,1536]{1,0:T(8,128)S(1)} %get-tuple-element.605, pred[]{:T(512)S(6)} %compare.33), kind=kOutput, calls=%fused_computation.7.clone.1 | convolution fusion | flops 2419261440 | bytes 1318913 | tf_op jit(solution)/shard_map/while/body/eval_jaxpr/dot_general | solution.py:33
  21.8 4.9 %fusion.59 = f32[64,1536]{1,0:T(8,128)S(1)} fusion(f32[2048,64]{0,1:T(8,128)S(1)} %bitcast.59, s32[2048]{0:T(1024)S(1)} %dynamic_slice.94, f32[64,1536]{1,0:T(8,128)S(1)} %get-tuple-element.605, pred[]{:T(512)S(6)} %compare.33), kind=kOutput, calls=%fused_computation.7.clone.1 | convolution fusion | flops 2419261440 | bytes 1318913 | tf_op jit(solution)/shard_map/while/body/eval_jaxpr/dot_general | solution.py:33
  26.9 4.9 %fusion.59 = f32[64,1536]{1,0:T(8,128)S(1)} fusion(f32[2048,64]{0,1:T(8,128)S(1)} %bitcast.59, s32[2048]{0:T(1024)S(1)} %dynamic_slice.94, f32[64,1536]{1,0:T(8,128)S(1)} %get-tuple-element.605, pred[]{:T(512)S(6)} %compare.33), kind=kOutput, calls=%fused_computation.7.clone.1 | convolution fusion | flops 2419261440 | bytes 1318913 | tf_op jit(solution)/shard_map/while/body/eval_jaxpr/dot_general | solution.py:33
  32.6 8.3 %all-to-all-start = ((s32[1,16,1536]{2,0,1:T(1,128)}), s32[1,16,1536]{2,0,1:T(1,128)S(1)}, u32[]{:S(2)}, u32[]{:S(2)}) async-start(s32[1,16,1536]{2,0,1:T(1,128)} %convert_element_type.35), calls=%async_computation | async-start | bytes 196608 | tf_op jit(solution)/shard_map/all_to_all | solution.py:91
  41.9 6.7 %all-to-all-done = s32[1,16,1536]{2,0,1:T(1,128)S(1)} async-done(((s32[1,16,1536]{2,0,1:T(1,128)}), s32[1,16,1536]{2,0,1:T(1,128)S(1)}, u32[]{:S(2)}, u32[]{:S(2)}) %all-to-all-start) | async-done | bytes 98336 | tf_op jit(solution)/shard_map/all_to_all | solution.py:91
  52.4 11.2 %all-to-all-done.1 = f32[3,16,1536]{2,0,1:T(4,128)S(1)} async-done(((f32[3,16,1536]{2,0,1:T(4,128)}), f32[3,16,1536]{2,0,1:T(4,128)S(1)}, u32[]{:S(2)}, u32[]{:S(2)}) %all-to-all-start.1) | async-done | bytes 294944 | tf_op jit(solution)/shard_map/all_to_all | solution.py:90
  63.7 87.0 %while.35 = (s32[]{:T(128)}, f32[204,128]{1,0:T(8,128)S(1)}, f32[204]{0:T(256)S(1)}, s32[24576]{0:T(1024)S(1)}, f32[24576]{0:T(1024)S(1)}, /*index=5*/s32[24576]...) while((s32[]{:T(128)}, f32[204,128]{1,0:T(8,128)S(1)}, ...), condition=%wide.region_6.7_spmd.clone.clone, body=%wide.region_5.6_spmd.clone.clone.sunk | while | flops 648760704 | bytes 15973794 | solution.py:135
  65.6 3.9 %convolution_add_fusion.3 = f32[204,128]{1,0:T(8,128)S(1)} fusion(f32[2048,204]{0,1:T(8,128)} %mul.212, f32[2048]{0:T(1024)S(1)} %get-tuple-element.592, s32[2048]{0:T(1024)S(1)} %broadcast_add_fusion.5, f32[2048]{0:T(1024)S(1)} %broadcast_subtract_fusion.3, s32[2048]{0:T(1024)S(1)} %get-tuple-element.593, f32[204,128]{1,0:T(8,128)S(1)} %get-tuple-element.636, ...), kind=kOutput, calls=%fused_computation.14.clone.1 | convolution fusion | flops 643091456 | bytes 1912833 | tf_op jit(solution)/shard_map/while/body/eval_jaxpr/dot_general | solution.py:33
  72.9 3.9 %convolution_add_fusion.3 = f32[204,128]{1,0:T(8,128)S(1)} fusion(f32[2048,204]{0,1:T(8,128)} %mul.212, f32[2048]{0:T(1024)S(1)} %get-tuple-element.592, s32[2048]{0:T(1024)S(1)} %broadcast_add_fusion.5, f32[2048]{0:T(1024)S(1)} %broadcast_subtract_fusion.3, s32[2048]{0:T(1024)S(1)} %get-tuple-element.593, f32[204,128]{1,0:T(8,128)S(1)} %get-tuple-element.636, ...), kind=kOutput, calls=%fused_computation.14.clone.1 | convolution fusion | flops 643091456 | bytes 1912833 | tf_op jit(solution)/shard_map/while/body/eval_jaxpr/dot_general | solution.py:33
  80.1 3.9 %convolution_add_fusion.3 = f32[204,128]{1,0:T(8,128)S(1)} fusion(f32[2048,204]{0,1:T(8,128)} %mul.212, f32[2048]{0:T(1024)S(1)} %get-tuple-element.592, s32[2048]{0:T(1024)S(1)} %broadcast_add_fusion.5, f32[2048]{0:T(1024)S(1)} %broadcast_subtract_fusion.3, s32[2048]{0:T(1024)S(1)} %get-tuple-element.593, f32[204,128]{1,0:T(8,128)S(1)} %get-tuple-element.636, ...), kind=kOutput, calls=%fused_computation.14.clone.1 | convolution fusion | flops 643091456 | bytes 1912833 | tf_op jit(solution)/shard_map/while/body/eval_jaxpr/dot_general | solution.py:33
  87.4 3.9 %convolution_add_fusion.3 = f32[204,128]{1,0:T(8,128)S(1)} fusion(f32[2048,204]{0,1:T(8,128)} %mul.212, f32[2048]{0:T(1024)S(1)} %get-tuple-element.592, s32[2048]{0:T(1024)S(1)} %broadcast_add_fusion.5, f32[2048]{0:T(1024)S(1)} %broadcast_subtract_fusion.3, s32[2048]{0:T(1024)S(1)} %get-tuple-element.593, f32[204,128]{1,0:T(8,128)S(1)} %get-tuple-element.636, ...), kind=kOutput, calls=%fused_computation.14.clone.1 | convolution fusion | flops 643091456 | bytes 1912833 | tf_op jit(solution)/shard_map/while/body/eval_jaxpr/dot_general | solution.py:33
  94.6 3.9 %convolution_add_fusion.3 = f32[204,128]{1,0:T(8,128)S(1)} fusion(f32[2048,204]{0,1:T(8,128)} %mul.212, f32[2048]{0:T(1024)S(1)} %get-tuple-element.592, s32[2048]{0:T(1024)S(1)} %broadcast_add_fusion.5, f32[2048]{0:T(1024)S(1)} %broadcast_subtract_fusion.3, s32[2048]{0:T(1024)S(1)} %get-tuple-element.593, f32[204,128]{1,0:T(8,128)S(1)} %get-tuple-element.636, ...), kind=kOutput, calls=%fused_computation.14.clone.1 | convolution fusion | flops 643091456 | bytes 1912833 | tf_op jit(solution)/shard_map/while/body/eval_jaxpr/dot_general | solution.py:33
  101.9 3.9 %convolution_add_fusion.3 = f32[204,128]{1,0:T(8,128)S(1)} fusion(f32[2048,204]{0,1:T(8,128)} %mul.212, f32[2048]{0:T(1024)S(1)} %get-tuple-element.592, s32[2048]{0:T(1024)S(1)} %broadcast_add_fusion.5, f32[2048]{0:T(1024)S(1)} %broadcast_subtract_fusion.3, s32[2048]{0:T(1024)S(1)} %get-tuple-element.593, f32[204,128]{1,0:T(8,128)S(1)} %get-tuple-element.636, ...), kind=kOutput, calls=%fused_computation.14.clone.1 | convolution fusion | flops 643091456 | bytes 1912833 | tf_op jit(solution)/shard_map/while/body/eval_jaxpr/dot_general | solution.py:33
  109.1 3.9 %convolution_add_fusion.3 = f32[204,128]{1,0:T(8,128)S(1)} fusion(f32[2048,204]{0,1:T(8,128)} %mul.212, f32[2048]{0:T(1024)S(1)} %get-tuple-element.592, s32[2048]{0:T(1024)S(1)} %broadcast_add_fusion.5, f32[2048]{0:T(1024)S(1)} %broadcast_subtract_fusion.3, s32[2048]{0:T(1024)S(1)} %get-tuple-element.593, f32[204,128]{1,0:T(8,128)S(1)} %get-tuple-element.636, ...), kind=kOutput, calls=%fused_computation.14.clone.1 | convolution fusion | flops 643091456 | bytes 1912833 | tf_op jit(solution)/shard_map/while/body/eval_jaxpr/dot_general | solution.py:33
  116.4 3.9 %convolution_add_fusion.3 = f32[204,128]{1,0:T(8,128)S(1)} fusion(f32[2048,204]{0,1:T(8,128)} %mul.212, f32[2048]{0:T(1024)S(1)} %get-tuple-element.592, s32[2048]{0:T(1024)S(1)} %broadcast_add_fusion.5, f32[2048]{0:T(1024)S(1)} %broadcast_subtract_fusion.3, s32[2048]{0:T(1024)S(1)} %get-tuple-element.593, f32[204,128]{1,0:T(8,128)S(1)} %get-tuple-element.636, ...), kind=kOutput, calls=%fused_computation.14.clone.1 | convolution fusion | flops 643091456 | bytes 1912833 | tf_op jit(solution)/shard_map/while/body/eval_jaxpr/dot_general | solution.py:33
  123.6 3.9 %convolution_add_fusion.3 = f32[204,128]{1,0:T(8,128)S(1)} fusion(f32[2048,204]{0,1:T(8,128)} %mul.212, f32[2048]{0:T(1024)S(1)} %get-tuple-element.592, s32[2048]{0:T(1024)S(1)} %broadcast_add_fusion.5, f32[2048]{0:T(1024)S(1)} %broadcast_subtract_fusion.3, s32[2048]{0:T(1024)S(1)} %get-tuple-element.593, f32[204,128]{1,0:T(8,128)S(1)} %get-tuple-element.636, ...), kind=kOutput, calls=%fused_computation.14.clone.1 | convolution fusion | flops 643091456 | bytes 1912833 | tf_op jit(solution)/shard_map/while/body/eval_jaxpr/dot_general | solution.py:33
  130.9 3.9 %convolution_add_fusion.3 = f32[204,128]{1,0:T(8,128)S(1)} fusion(f32[2048,204]{0,1:T(8,128)} %mul.212, f32[2048]{0:T(1024)S(1)} %get-tuple-element.592, s32[2048]{0:T(1024)S(1)} %broadcast_add_fusion.5, f32[2048]{0:T(1024)S(1)} %broadcast_subtract_fusion.3, s32[2048]{0:T(1024)S(1)} %get-tuple-element.593, f32[204,128]{1,0:T(8,128)S(1)} %get-tuple-element.636, ...), kind=kOutput, calls=%fused_computation.14.clone.1 | convolution fusion | flops 643091456 | bytes 1912833 | tf_op jit(solution)/shard_map/while/body/eval_jaxpr/dot_general | solution.py:33
  138.1 3.9 %convolution_add_fusion.3 = f32[204,128]{1,0:T(8,128)S(1)} fusion(f32[2048,204]{0,1:T(8,128)} %mul.212, f32[2048]{0:T(1024)S(1)} %get-tuple-element.592, s32[2048]{0:T(1024)S(1)} %broadcast_add_fusion.5, f32[2048]{0:T(1024)S(1)} %broadcast_subtract_fusion.3, s32[2048]{0:T(1024)S(1)} %get-tuple-element.593, f32[204,128]{1,0:T(8,128)S(1)} %get-tuple-element.636, ...), kind=kOutput, calls=%fused_computation.14.clone.1 | convolution fusion | flops 643091456 | bytes 1912833 | tf_op jit(solution)/shard_map/while/body/eval_jaxpr/dot_general | solution.py:33
  145.4 3.9 %convolution_add_fusion.3 = f32[204,128]{1,0:T(8,128)S(1)} fusion(f32[2048,204]{0,1:T(8,128)} %mul.212, f32[2048]{0:T(1024)S(1)} %get-tuple-element.592, s32[2048]{0:T(1024)S(1)} %broadcast_add_fusion.5, f32[2048]{0:T(1024)S(1)} %broadcast_subtract_fusion.3, s32[2048]{0:T(1024)S(1)} %get-tuple-element.593, f32[204,128]{1,0:T(8,128)S(1)} %get-tuple-element.636, ...), kind=kOutput, calls=%fused_computation.14.clone.1 | convolution fusion | flops 643091456 | bytes 1912833 | tf_op jit(solution)/shard_map/while/body/eval_jaxpr/dot_general | solution.py:33
  160.4 19.5 %all-reduce.2.cloned.1.call-done = f32[6,2,16,128]{3,2,1,0:T(8,128)} async-done(((f32[6,2,16,128]{3,2,1,0:T(8,128)}), f32[6,2,16,128]{3,2,1,0:T(8,128)}) %all-reduce.2.cloned.1.call-update) | async-done | bytes 98320 | tf_op jit(solution)/shard_map/psum | solution.py:145
  186.7 4.2 %collective-permute-done.3 = f32[40,2,1,128]{3,0,2,1:T(8,128)S(1)} collective-permute-done((f32[40,2,1,128]{3,0,2,1:T(8,128)S(1)}, f32[40,2,1,128]{3,0,2,1:T(8,128)S(1)}, u32[]{:S(2)}, u32[]{:S(2)}) %collective-permute-start.3) | collective-permute-done | bytes 40992 | tf_op jit(solution)/shard_map/ppermute | solution.py:22
  197.7 3.8 %collective-permute-done.5 = f32[40,2,18,1]{0,2,3,1:T(8,128)S(1)} collective-permute-done((f32[40,2,18,1]{0,2,3,1:T(8,128)S(1)}, f32[40,2,18,1]{0,2,3,1:T(8,128)S(1)}, u32[]{:S(2)}, u32[]{:S(2)}) %collective-permute-start.5) | collective-permute-done | bytes 5792 | tf_op jit(solution)/shard_map/ppermute | solution.py:22
  (259 shorter events, 74.5 us)
Async XLA Ops:
  6.5 4.8 %copy-start.2 = (s32[8192]{0:T(1024)S(1)}, s32[8192]{0:T(1024)}, u32[]{:S(2)}) copy-start(s32[8192]{0:T(1024)} %param.19) | copy-start | bytes 98308
  6.5 4.8 %copy-start.3 = (s32[8192]{0:T(1024)S(1)}, s32[8192]{0:T(1024)}, u32[]{:S(2)}) copy-start(s32[8192]{0:T(1024)} %param.20) | copy-start | bytes 98308
  6.5 4.8 %copy-start.4 = (f32[8192]{0:T(1024)S(1)}, f32[8192]{0:T(1024)}, u32[]{:S(2)}) copy-start(f32[8192]{0:T(1024)} %param.17) | copy-start | bytes 98308
  32.6 16.0 %all-to-all-start = ((s32[1,16,1536]{2,0,1:T(1,128)}), s32[1,16,1536]{2,0,1:T(1,128)S(1)}, u32[]{:S(2)}, u32[]{:S(2)}) async-start(s32[1,16,1536]{2,0,1:T(1,128)} %convert_element_type.35), calls=%async_computation | async-start | bytes 196608 | tf_op jit(solution)/shard_map/all_to_all | solution.py:91
  48.6 14.9 %all-to-all-start.1 = ((f32[3,16,1536]{2,0,1:T(4,128)}), f32[3,16,1536]{2,0,1:T(4,128)S(1)}, u32[]{:S(2)}, u32[]{:S(2)}) async-start(f32[3,16,1536]{2,0,1:T(4,128)} %copy.54), calls=%async_computation.1 | async-start | bytes 786432 | tf_op jit(solution)/shard_map/all_to_all | solution.py:90
  52.1 127.7 %all-reduce.2.cloned.1.call-start = ((), (), s32[]{:S(2)}) async-start(), calls=%async_computation.2 | async-start | bytes 196608 | tf_op jit(solution)/shard_map/psum | solution.py:145
  72.8 3.9 %copy-start = (f32[2048,204]{0,1:T(8,128)S(1)}, f32[2048,204]{0,1:T(8,128)}, u32[]{:S(2)}) copy-start(f32[2048,204]{0,1:T(8,128)} %mul.212) | copy-start | bytes 5013508 | tf_op jit(solution)/shard_map/while
  80.1 3.9 %copy-start = (f32[2048,204]{0,1:T(8,128)S(1)}, f32[2048,204]{0,1:T(8,128)}, u32[]{:S(2)}) copy-start(f32[2048,204]{0,1:T(8,128)} %mul.212) | copy-start | bytes 5013508 | tf_op jit(solution)/shard_map/while
  87.3 3.9 %copy-start = (f32[2048,204]{0,1:T(8,128)S(1)}, f32[2048,204]{0,1:T(8,128)}, u32[]{:S(2)}) copy-start(f32[2048,204]{0,1:T(8,128)} %mul.212) | copy-start | bytes 5013508 | tf_op jit(solution)/shard_map/while
  94.6 3.9 %copy-start = (f32[2048,204]{0,1:T(8,128)S(1)}, f32[2048,204]{0,1:T(8,128)}, u32[]{:S(2)}) copy-start(f32[2048,204]{0,1:T(8,128)} %mul.212) | copy-start | bytes 5013508 | tf_op jit(solution)/shard_map/while
  101.8 3.9 %copy-start = (f32[2048,204]{0,1:T(8,128)S(1)}, f32[2048,204]{0,1:T(8,128)}, u32[]{:S(2)}) copy-start(f32[2048,204]{0,1:T(8,128)} %mul.212) | copy-start | bytes 5013508 | tf_op jit(solution)/shard_map/while
  109.1 3.9 %copy-start = (f32[2048,204]{0,1:T(8,128)S(1)}, f32[2048,204]{0,1:T(8,128)}, u32[]{:S(2)}) copy-start(f32[2048,204]{0,1:T(8,128)} %mul.212) | copy-start | bytes 5013508 | tf_op jit(solution)/shard_map/while
  116.3 3.9 %copy-start = (f32[2048,204]{0,1:T(8,128)S(1)}, f32[2048,204]{0,1:T(8,128)}, u32[]{:S(2)}) copy-start(f32[2048,204]{0,1:T(8,128)} %mul.212) | copy-start | bytes 5013508 | tf_op jit(solution)/shard_map/while
  123.6 3.9 %copy-start = (f32[2048,204]{0,1:T(8,128)S(1)}, f32[2048,204]{0,1:T(8,128)}, u32[]{:S(2)}) copy-start(f32[2048,204]{0,1:T(8,128)} %mul.212) | copy-start | bytes 5013508 | tf_op jit(solution)/shard_map/while
  130.9 3.9 %copy-start = (f32[2048,204]{0,1:T(8,128)S(1)}, f32[2048,204]{0,1:T(8,128)}, u32[]{:S(2)}) copy-start(f32[2048,204]{0,1:T(8,128)} %mul.212) | copy-start | bytes 5013508 | tf_op jit(solution)/shard_map/while
  138.1 3.9 %copy-start = (f32[2048,204]{0,1:T(8,128)S(1)}, f32[2048,204]{0,1:T(8,128)}, u32[]{:S(2)}) copy-start(f32[2048,204]{0,1:T(8,128)} %mul.212) | copy-start | bytes 5013508 | tf_op jit(solution)/shard_map/while
  145.4 3.9 %copy-start = (f32[2048,204]{0,1:T(8,128)S(1)}, f32[2048,204]{0,1:T(8,128)}, u32[]{:S(2)}) copy-start(f32[2048,204]{0,1:T(8,128)} %mul.212) | copy-start | bytes 5013508 | tf_op jit(solution)/shard_map/while
  150.7 29.1 %copy-start.1 = (bf16[40,6,2,16,128]{4,3,2,1,0:T(8,128)(2,1)S(1)}, bf16[40,6,2,16,128]{4,3,2,1,0:T(8,128)(2,1)}, u32[]{:S(2)}) copy-start(bf16[40,6,2,16,128]{4,3,2,1,0:T(8,128)(2,1)} %param.23) | copy-start | bytes 5898244
  150.8 3.9 %collective-permute-start = (f32[12,17]{1,0:T(8,128)S(1)}, f32[12,17]{1,0:T(8,128)S(1)}, u32[]{:S(2)}, u32[]{:S(2)}) collective-permute-start(f32[12,17]{1,0:T(8,128)S(1)} %reshape.290), channel_id=1, source_target_pairs={{0,2},{1,3},{4,6},{5,7},{8,10},{9,11},{12,14},{13,15},{16,18},{17,... | collective-permute-start | bytes 2456 | tf_op jit(solution)/shard_map/ppermute | solution.py:11
  155.5 4.1 %collective-permute-start.1 = (f32[12,128]{1,0:T(8,128)S(1)}, f32[12,128]{1,0:T(8,128)S(1)}, u32[]{:S(2)}, u32[]{:S(2)}) collective-permute-start(f32[12,128]{1,0:T(8,128)S(1)} %scatter-add.11), channel_id=1, source_target_pairs={{0,4},{4,8},{8,12},{12,16},{16,20},{20,24},{24,28},{1,5},{5,9},{9,... | collective-permute-start | bytes 18440 | tf_op jit(solution)/shard_map/ppermute | solution.py:11
  181.3 5.3 %collective-permute-start.2 = (f32[40,2,1,128]{3,0,2,1:T(8,128)S(1)}, f32[40,2,1,128]{3,0,2,1:T(8,128)S(1)}, u32[]{:S(2)}, u32[]{:S(2)}) collective-permute-start(f32[40,2,1,128]{3,0,2,1:T(8,128)S(1)} %copy.61), channel_id=1, source_target_pairs={{0,4},{4,8},{8,12},{12,16},{16,20},{20,24},{24,28},{1,5},{5,9},{9,... | collective-permute-start | bytes 122888 | tf_op jit(solution)/shard_map/ppermute | solution.py:21
  185.0 5.9 %collective-permute-start.3 = (f32[40,2,1,128]{3,0,2,1:T(8,128)S(1)}, f32[40,2,1,128]{3,0,2,1:T(8,128)S(1)}, u32[]{:S(2)}, u32[]{:S(2)}) collective-permute-start(f32[40,2,1,128]{3,0,2,1:T(8,128)S(1)} %copy.62), channel_id=1, source_target_pairs={{4,0},{8,4},{12,8},{16,12},{20,16},{24,20},{28,24},{5,1},{9,5},{13... | collective-permute-start | bytes 122888 | tf_op jit(solution)/shard_map/ppermute | solution.py:22
  191.9 5.4 %collective-permute-start.4 = (f32[40,2,18,1]{0,2,3,1:T(8,128)S(1)}, f32[40,2,18,1]{0,2,3,1:T(8,128)S(1)}, u32[]{:S(2)}, u32[]{:S(2)}) collective-permute-start(f32[40,2,18,1]{0,2,3,1:T(8,128)S(1)} %copy.65), channel_id=1, source_target_pairs={{0,2},{1,3},{4,6},{5,7},{8,10},{9,11},{12,14},{13,15},{16,18},{17,... | collective-permute-start | bytes 17288 | tf_op jit(solution)/shard_map/ppermute | solution.py:21
  195.8 5.7 %collective-permute-start.5 = (f32[40,2,18,1]{0,2,3,1:T(8,128)S(1)}, f32[40,2,18,1]{0,2,3,1:T(8,128)S(1)}, u32[]{:S(2)}, u32[]{:S(2)}) collective-permute-start(f32[40,2,18,1]{0,2,3,1:T(8,128)S(1)} %copy.66), channel_id=1, source_target_pairs={{2,0},{3,1},{6,4},{7,5},{10,8},{11,9},{14,12},{15,13},{18,16},{19,... | collective-permute-start | bytes 17288 | tf_op jit(solution)/shard_map/ppermute | solution.py:22
  (1 other events, 3.9 us)
Sparse Core Ops, SparseCore 0:
  160.5 19.3 all-reduce.1
where the time goes:
time: 211 us
  matrix products  84.9 us (40%)
  waiting for transfers between devices  47.1 us (22%)
  starting transfers between devices  26.9 us (13%)
  local copies, waits for them, and re-layouts  24.9 us (12%)
  between operations  14.4 us (7%)
  other arithmetic  11 us (5%)
    dot_general x28, matrix products, contract_rows(): lax.dot_general(left, right, (((0,), (0,)), ((), ())), precision=lax.Prec...  83.7 us
    psum x1, waiting for transfers between devices, body(): grad = lax.psum(interior, 'mem')  19.5 us
    mul x12, local copies, waits for them, and re-layouts, spread_rows(): layer_hot[:, :, None] * weight_x[:, None, :]  17.2 us
    all_to_all x1, waiting for transfers between devices, body(): lax.all_to_all(send_floats, ('tx', 'ty'), split_axis=1, concat_axis=1, ti...  11.2 us
    all_to_all x1, starting transfers between devices, body(): lax.all_to_all(send_index, ('tx', 'ty'), split_axis=1, concat_axis=1, til...  8.34 us
    ppermute x2, waiting for transfers between devices, extended_2(): after = lax.ppermute(initial, axis, down)  8.04 us
    ppermute x2, starting transfers between devices, extended_2(): before = lax.ppermute(last, axis, up)  7.05 us
    all_to_all x1, waiting for transfers between devices, body(): lax.all_to_all(send_index, ('tx', 'ty'), split_axis=1, concat_axis=1, til...  6.68 us
  transfers between devices with their start and end apart: 9, of which 8 were waited for; matrix products, arithmetic and copies ran while one was open for 2% of the time, Pallas kernels for 0%

commit v1 on v0

--- a/solution.py
+++ b/solution.py
@@ -142,7 +142,7 @@
     east_rim = east_rim.at[:, 0].add(from_south[:, cells_x])
     from_west = shifted(east_rim, "tx", 1)
     interior = interior.at[:, 0, :].add(from_west)
-    grad = lax.psum(interior, "mem")
+    grad = jnp.sum(lax.all_gather(interior, "mem"), axis=0)
     grad_slots = grad.reshape(slot_count, level_count, cells_x, cells_y)
     contrib = jnp.sum(ensemble * grad_slots[None], axis=1)
     padded = extended_2(contrib, (("tx", 2), ("ty", 3)), 1)

time: 211 us -> 181 us (0.86)
  waiting for transfers between devices: 47.1 us -> 28.3 us
  between operations: 14.4 us -> 1.06 us
  blocking collectives: 0 us -> 2.13 us
    psum x1 -> x0, waiting for transfers between devices: 19.5 us -> none  [body(): grad = lax.psum(interior, 'mem')]
    all_gather x0 -> x1, blocking collectives: none -> 2.13 us  [body(): grad = jnp.sum(lax.all_gather(interior, 'mem'), axis=0)]
  transfers between devices with their start and end apart: 9 -> 8, of which waited for: 8 -> 7; matrix products, arithmetic and copies ran while one was open for 2% -> 2% of each run, Pallas kernels for 0% -> 0%
where the time goes in v1:
time: 181 us; the launch traced here: 180 us
  matrix products  84.9 us (47%)
  waiting for transfers between devices  28.3 us (16%)
  starting transfers between devices  28.2 us (16%)
  local copies, waits for them, and re-layouts  24.1 us (13%)
  other arithmetic  10.1 us (6%)
  blocking collectives  2.13 us (1%)
    dot_general x28, matrix products, contract_rows(): lax.dot_general(left, right, (((0,), (0,)), ((), ())), precision=lax.Prec...  83.7 us
    mul x12, local copies, waits for them, and re-layouts, spread_rows(): layer_hot[:, :, None] * weight_x[:, None, :]  17.1 us
    all_to_all x1, waiting for transfers between devices, body(): lax.all_to_all(send_floats, ('tx', 'ty'), split_axis=1, concat_axis=1, ti...  11.2 us
    ppermute x2, waiting for transfers between devices, extended_2(): after = lax.ppermute(initial, axis, down)  8.62 us
    ppermute x2, starting transfers between devices, extended_2(): before = lax.ppermute(last, axis, up)  8.37 us
    all_to_all x1, starting transfers between devices, body(): lax.all_to_all(send_index, ('tx', 'ty'), split_axis=1, concat_axis=1, til...  8.36 us
    all_to_all x1, waiting for transfers between devices, body(): lax.all_to_all(send_index, ('tx', 'ty'), split_axis=1, concat_axis=1, til...  6.65 us
    ppermute x2, starting transfers between devices, shifted(): return lax.ppermute(block, axis, route)  5.36 us
  transfers between devices with their start and end apart: 8, of which 7 were waited for; matrix products, arithmetic and copies ran while one was open for 2% of the time, Pallas kernels for 0%

profile of v1, /device:TPU:0, one launch (start us, length us, event | category | flops | bytes accessed | tf_op | source)
XLA Modules:
  0.0 180.2 jit_solution(8685337742207349537)
XLA Ops:
  5.0 20.3 %while.34 = (s32[]{:T(128)}, f32[64,1536]{1,0:T(8,128)S(1)}, f32[8192,4]{0,1:T(4,128)S(1)}, f32[8192,16]{0,1:T(8,128)S(1)}, s32[8192]{0:T(1024)S(1)}, /*index=5*/s32[]{:T(128)}, s32[]{:T(128)}, s32[]{:T(128)}, s32[]{:T(128)}) while((s32[]{:T(128)}, f32[64,1536]{1,0:T(8,128)S(1)}, f32[8192,4]{0,1:T(4,128)S(1)}, ...), condition=%wide.region_4.5_spmd.clone, body=%wide.region_3.4_spmd.clone.sunk | while | flops 2419392512 | bytes 2351265 | solution.py:83
  5.1 4.9 %fusion.60 = f32[64,1536]{1,0:T(8,128)S(1)} fusion(f32[2048,64]{0,1:T(8,128)S(1)} %bitcast.64, s32[2048]{0:T(1024)S(1)} %dynamic_slice.94, f32[64,1536]{1,0:T(8,128)S(1)} %get-tuple-element.605, pred[]{:T(512)S(6)} %compare.33), kind=kOutput, calls=%fused_computation.7.clone.1 | convolution fusion | flops 2419261440 | bytes 1318913 | tf_op jit(solution)/shard_map/while/body/eval_jaxpr/dot_general | solution.py:33
  10.2 4.9 %fusion.60 = f32[64,1536]{1,0:T(8,128)S(1)} fusion(f32[2048,64]{0,1:T(8,128)S(1)} %bitcast.64, s32[2048]{0:T(1024)S(1)} %dynamic_slice.94, f32[64,1536]{1,0:T(8,128)S(1)} %get-tuple-element.605, pred[]{:T(512)S(6)} %compare.33), kind=kOutput, calls=%fused_computation.7.clone.1 | convolution fusion | flops 2419261440 | bytes 1318913 | tf_op jit(solution)/shard_map/while/body/eval_jaxpr/dot_general | solution.py:33
  15.3 4.9 %fusion.60 = f32[64,1536]{1,0:T(8,128)S(1)} fusion(f32[2048,64]{0,1:T(8,128)S(1)} %bitcast.64, s32[2048]{0:T(1024)S(1)} %dynamic_slice.94, f32[64,1536]{1,0:T(8,128)S(1)} %get-tuple-element.605, pred[]{:T(512)S(6)} %compare.33), kind=kOutput, calls=%fused_computation.7.clone.1 | convolution fusion | flops 2419261440 | bytes 1318913 | tf_op jit(solution)/shard_map/while/body/eval_jaxpr/dot_general | solution.py:33
  20.4 4.9 %fusion.60 = f32[64,1536]{1,0:T(8,128)S(1)} fusion(f32[2048,64]{0,1:T(8,128)S(1)} %bitcast.64, s32[2048]{0:T(1024)S(1)} %dynamic_slice.94, f32[64,1536]{1,0:T(8,128)S(1)} %get-tuple-element.605, pred[]{:T(512)S(6)} %compare.33), kind=kOutput, calls=%fused_computation.7.clone.1 | convolution fusion | flops 2419261440 | bytes 1318913 | tf_op jit(solution)/shard_map/while/body/eval_jaxpr/dot_general | solution.py:33
  26.0 8.4 %all-to-all-start = ((s32[1,16,1536]{2,0,1:T(1,128)}), s32[1,16,1536]{2,0,1:T(1,128)S(1)}, u32[]{:S(2)}, u32[]{:S(2)}) async-start(s32[1,16,1536]{2,0,1:T(1,128)} %convert_element_type.35), calls=%async_computation | async-start | bytes 196608 | tf_op jit(solution)/shard_map/all_to_all | solution.py:91
  35.4 6.7 %all-to-all-done = s32[1,16,1536]{2,0,1:T(1,128)S(1)} async-done(((s32[1,16,1536]{2,0,1:T(1,128)}), s32[1,16,1536]{2,0,1:T(1,128)S(1)}, u32[]{:S(2)}, u32[]{:S(2)}) %all-to-all-start) | async-done | bytes 98336 | tf_op jit(solution)/shard_map/all_to_all | solution.py:91
  45.8 11.2 %all-to-all-done.1 = f32[3,16,1536]{2,0,1:T(4,128)S(1)} async-done(((f32[3,16,1536]{2,0,1:T(4,128)}), f32[3,16,1536]{2,0,1:T(4,128)S(1)}, u32[]{:S(2)}, u32[]{:S(2)}) %all-to-all-start.1) | async-done | bytes 294944 | tf_op jit(solution)/shard_map/all_to_all | solution.py:90
  57.2 86.9 %while.35 = (s32[]{:T(128)}, f32[204,128]{1,0:T(8,128)S(1)}, f32[204]{0:T(256)S(1)}, s32[24576]{0:T(1024)S(1)}, f32[24576]{0:T(1024)S(1)}, /*index=5*/s32[24576]...) while((s32[]{:T(128)}, f32[204,128]{1,0:T(8,128)S(1)}, ...), condition=%wide.region_6.7_spmd.clone.clone, body=%wide.region_5.6_spmd.clone.clone.sunk | while | flops 648760704 | bytes 15973794 | solution.py:135
  59.1 3.9 %convolution_add_fusion.3 = f32[204,128]{1,0:T(8,128)S(1)} fusion(f32[2048,204]{0,1:T(8,128)} %mul.212, f32[2048]{0:T(1024)S(1)} %get-tuple-element.592, s32[2048]{0:T(1024)S(1)} %broadcast_add_fusion.5, f32[2048]{0:T(1024)S(1)} %broadcast_subtract_fusion.3, s32[2048]{0:T(1024)S(1)} %get-tuple-element.593, f32[204,128]{1,0:T(8,128)S(1)} %get-tuple-element.636, ...), kind=kOutput, calls=%fused_computation.14.clone.1 | convolution fusion | flops 643091456 | bytes 1912833 | tf_op jit(solution)/shard_map/while/body/eval_jaxpr/dot_general | solution.py:33
  66.3 3.9 %convolution_add_fusion.3 = f32[204,128]{1,0:T(8,128)S(1)} fusion(f32[2048,204]{0,1:T(8,128)} %mul.212, f32[2048]{0:T(1024)S(1)} %get-tuple-element.592, s32[2048]{0:T(1024)S(1)} %broadcast_add_fusion.5, f32[2048]{0:T(1024)S(1)} %broadcast_subtract_fusion.3, s32[2048]{0:T(1024)S(1)} %get-tuple-element.593, f32[204,128]{1,0:T(8,128)S(1)} %get-tuple-element.636, ...), kind=kOutput, calls=%fused_computation.14.clone.1 | convolution fusion | flops 643091456 | bytes 1912833 | tf_op jit(solution)/shard_map/while/body/eval_jaxpr/dot_general | solution.py:33
  73.6 3.9 %convolution_add_fusion.3 = f32[204,128]{1,0:T(8,128)S(1)} fusion(f32[2048,204]{0,1:T(8,128)} %mul.212, f32[2048]{0:T(1024)S(1)} %get-tuple-element.592, s32[2048]{0:T(1024)S(1)} %broadcast_add_fusion.5, f32[2048]{0:T(1024)S(1)} %broadcast_subtract_fusion.3, s32[2048]{0:T(1024)S(1)} %get-tuple-element.593, f32[204,128]{1,0:T(8,128)S(1)} %get-tuple-element.636, ...), kind=kOutput, calls=%fused_computation.14.clone.1 | convolution fusion | flops 643091456 | bytes 1912833 | tf_op jit(solution)/shard_map/while/body/eval_jaxpr/dot_general | solution.py:33
  80.8 3.9 %convolution_add_fusion.3 = f32[204,128]{1,0:T(8,128)S(1)} fusion(f32[2048,204]{0,1:T(8,128)} %mul.212, f32[2048]{0:T(1024)S(1)} %get-tuple-element.592, s32[2048]{0:T(1024)S(1)} %broadcast_add_fusion.5, f32[2048]{0:T(1024)S(1)} %broadcast_subtract_fusion.3, s32[2048]{0:T(1024)S(1)} %get-tuple-element.593, f32[204,128]{1,0:T(8,128)S(1)} %get-tuple-element.636, ...), kind=kOutput, calls=%fused_computation.14.clone.1 | convolution fusion | flops 643091456 | bytes 1912833 | tf_op jit(solution)/shard_map/while/body/eval_jaxpr/dot_general | solution.py:33
  88.0 3.9 %convolution_add_fusion.3 = f32[204,128]{1,0:T(8,128)S(1)} fusion(f32[2048,204]{0,1:T(8,128)} %mul.212, f32[2048]{0:T(1024)S(1)} %get-tuple-element.592, s32[2048]{0:T(1024)S(1)} %broadcast_add_fusion.5, f32[2048]{0:T(1024)S(1)} %broadcast_subtract_fusion.3, s32[2048]{0:T(1024)S(1)} %get-tuple-element.593, f32[204,128]{1,0:T(8,128)S(1)} %get-tuple-element.636, ...), kind=kOutput, calls=%fused_computation.14.clone.1 | convolution fusion | flops 643091456 | bytes 1912833 | tf_op jit(solution)/shard_map/while/body/eval_jaxpr/dot_general | solution.py:33
  95.3 3.9 %convolution_add_fusion.3 = f32[204,128]{1,0:T(8,128)S(1)} fusion(f32[2048,204]{0,1:T(8,128)} %mul.212, f32[2048]{0:T(1024)S(1)} %get-tuple-element.592, s32[2048]{0:T(1024)S(1)} %broadcast_add_fusion.5, f32[2048]{0:T(1024)S(1)} %broadcast_subtract_fusion.3, s32[2048]{0:T(1024)S(1)} %get-tuple-element.593, f32[204,128]{1,0:T(8,128)S(1)} %get-tuple-element.636, ...), kind=kOutput, calls=%fused_computation.14.clone.1 | convolution fusion | flops 643091456 | bytes 1912833 | tf_op jit(solution)/shard_map/while/body/eval_jaxpr/dot_general | solution.py:33
  102.5 3.9 %convolution_add_fusion.3 = f32[204,128]{1,0:T(8,128)S(1)} fusion(f32[2048,204]{0,1:T(8,128)} %mul.212, f32[2048]{0:T(1024)S(1)} %get-tuple-element.592, s32[2048]{0:T(1024)S(1)} %broadcast_add_fusion.5, f32[2048]{0:T(1024)S(1)} %broadcast_subtract_fusion.3, s32[2048]{0:T(1024)S(1)} %get-tuple-element.593, f32[204,128]{1,0:T(8,128)S(1)} %get-tuple-element.636, ...), kind=kOutput, calls=%fused_computation.14.clone.1 | convolution fusion | flops 643091456 | bytes 1912833 | tf_op jit(solution)/shard_map/while/body/eval_jaxpr/dot_general | solution.py:33
  109.8 3.9 %convolution_add_fusion.3 = f32[204,128]{1,0:T(8,128)S(1)} fusion(f32[2048,204]{0,1:T(8,128)} %mul.212, f32[2048]{0:T(1024)S(1)} %get-tuple-element.592, s32[2048]{0:T(1024)S(1)} %broadcast_add_fusion.5, f32[2048]{0:T(1024)S(1)} %broadcast_subtract_fusion.3, s32[2048]{0:T(1024)S(1)} %get-tuple-element.593, f32[204,128]{1,0:T(8,128)S(1)} %get-tuple-element.636, ...), kind=kOutput, calls=%fused_computation.14.clone.1 | convolution fusion | flops 643091456 | bytes 1912833 | tf_op jit(solution)/shard_map/while/body/eval_jaxpr/dot_general | solution.py:33
  117.0 3.9 %convolution_add_fusion.3 = f32[204,128]{1,0:T(8,128)S(1)} fusion(f32[2048,204]{0,1:T(8,128)} %mul.212, f32[2048]{0:T(1024)S(1)} %get-tuple-element.592, s32[2048]{0:T(1024)S(1)} %broadcast_add_fusion.5, f32[2048]{0:T(1024)S(1)} %broadcast_subtract_fusion.3, s32[2048]{0:T(1024)S(1)} %get-tuple-element.593, f32[204,128]{1,0:T(8,128)S(1)} %get-tuple-element.636, ...), kind=kOutput, calls=%fused_computation.14.clone.1 | convolution fusion | flops 643091456 | bytes 1912833 | tf_op jit(solution)/shard_map/while/body/eval_jaxpr/dot_general | solution.py:33
  124.3 3.9 %convolution_add_fusion.3 = f32[204,128]{1,0:T(8,128)S(1)} fusion(f32[2048,204]{0,1:T(8,128)} %mul.212, f32[2048]{0:T(1024)S(1)} %get-tuple-element.592, s32[2048]{0:T(1024)S(1)} %broadcast_add_fusion.5, f32[2048]{0:T(1024)S(1)} %broadcast_subtract_fusion.3, s32[2048]{0:T(1024)S(1)} %get-tuple-element.593, f32[204,128]{1,0:T(8,128)S(1)} %get-tuple-element.636, ...), kind=kOutput, calls=%fused_computation.14.clone.1 | convolution fusion | flops 643091456 | bytes 1912833 | tf_op jit(solution)/shard_map/while/body/eval_jaxpr/dot_general | solution.py:33
  131.5 3.9 %convolution_add_fusion.3 = f32[204,128]{1,0:T(8,128)S(1)} fusion(f32[2048,204]{0,1:T(8,128)} %mul.212, f32[2048]{0:T(1024)S(1)} %get-tuple-element.592, s32[2048]{0:T(1024)S(1)} %broadcast_add_fusion.5, f32[2048]{0:T(1024)S(1)} %broadcast_subtract_fusion.3, s32[2048]{0:T(1024)S(1)} %get-tuple-element.593, f32[204,128]{1,0:T(8,128)S(1)} %get-tuple-element.636, ...), kind=kOutput, calls=%fused_computation.14.clone.1 | convolution fusion | flops 643091456 | bytes 1912833 | tf_op jit(solution)/shard_map/while/body/eval_jaxpr/dot_general | solution.py:33
  138.7 3.9 %convolution_add_fusion.3 = f32[204,128]{1,0:T(8,128)S(1)} fusion(f32[2048,204]{0,1:T(8,128)} %mul.212, f32[2048]{0:T(1024)S(1)} %get-tuple-element.592, s32[2048]{0:T(1024)S(1)} %broadcast_add_fusion.5, f32[2048]{0:T(1024)S(1)} %broadcast_subtract_fusion.3, s32[2048]{0:T(1024)S(1)} %get-tuple-element.593, f32[204,128]{1,0:T(8,128)S(1)} %get-tuple-element.636, ...), kind=kOutput, calls=%fused_computation.14.clone.1 | convolution fusion | flops 643091456 | bytes 1912833 | tf_op jit(solution)/shard_map/while/body/eval_jaxpr/dot_general | solution.py:33
  155.8 4.2 %collective-permute-start.2 = (f32[40,2,1,128]{3,0,2,1:T(8,128)S(1)}, f32[40,2,1,128]{3,0,2,1:T(8,128)S(1)}, u32[]{:S(2)}, u32[]{:S(2)}) collective-permute-start(f32[40,2,1,128]{3,0,2,1:T(8,128)S(1)} %copy.66), channel_id=1, source_target_pairs={{0,4},{4,8},{8,12},{12,16},{16,20},{20,24},{24,28},{1,5},{5,9},{9,... | collective-permute-start | bytes 122888 | tf_op jit(solution)/shard_map/ppermute | solution.py:21
  161.7 4.8 %collective-permute-done.3 = f32[40,2,1,128]{3,0,2,1:T(8,128)S(1)} collective-permute-done((f32[40,2,1,128]{3,0,2,1:T(8,128)S(1)}, f32[40,2,1,128]{3,0,2,1:T(8,128)S(1)}, u32[]{:S(2)}, u32[]{:S(2)}) %collective-permute-start.3) | collective-permute-done | bytes 40992 | tf_op jit(solution)/shard_map/ppermute | solution.py:22
  167.5 4.2 %collective-permute-start.4 = (f32[40,2,18,1]{0,2,3,1:T(8,128)S(1)}, f32[40,2,18,1]{0,2,3,1:T(8,128)S(1)}, u32[]{:S(2)}, u32[]{:S(2)}) collective-permute-start(f32[40,2,18,1]{0,2,3,1:T(8,128)S(1)} %copy.70), channel_id=1, source_target_pairs={{0,2},{1,3},{4,6},{5,7},{8,10},{9,11},{12,14},{13,15},{16,18},{17,... | collective-permute-start | bytes 17288 | tf_op jit(solution)/shard_map/ppermute | solution.py:21
  (259 shorter events, 71.6 us)
Async XLA Ops:
  0.0 4.8 %copy-start.2 = (s32[8192]{0:T(1024)S(1)}, s32[8192]{0:T(1024)}, u32[]{:S(2)}) copy-start(s32[8192]{0:T(1024)} %param.19) | copy-start | bytes 98308
  0.0 4.8 %copy-start.3 = (s32[8192]{0:T(1024)S(1)}, s32[8192]{0:T(1024)}, u32[]{:S(2)}) copy-start(s32[8192]{0:T(1024)} %param.20) | copy-start | bytes 98308
  0.0 4.8 %copy-start.4 = (f32[8192]{0:T(1024)S(1)}, f32[8192]{0:T(1024)}, u32[]{:S(2)}) copy-start(f32[8192]{0:T(1024)} %param.17) | copy-start | bytes 98308
  26.0 16.0 %all-to-all-start = ((s32[1,16,1536]{2,0,1:T(1,128)}), s32[1,16,1536]{2,0,1:T(1,128)S(1)}, u32[]{:S(2)}, u32[]{:S(2)}) async-start(s32[1,16,1536]{2,0,1:T(1,128)} %convert_element_type.35), calls=%async_computation | async-start | bytes 196608 | tf_op jit(solution)/shard_map/all_to_all | solution.py:91
  42.1 14.9 %all-to-all-start.1 = ((f32[3,16,1536]{2,0,1:T(4,128)}), f32[3,16,1536]{2,0,1:T(4,128)S(1)}, u32[]{:S(2)}, u32[]{:S(2)}) async-start(f32[3,16,1536]{2,0,1:T(4,128)} %copy.57), calls=%async_computation.1 | async-start | bytes 786432 | tf_op jit(solution)/shard_map/all_to_all | solution.py:90
  59.1 3.9 %copy-start = (f32[2048,204]{0,1:T(8,128)S(1)}, f32[2048,204]{0,1:T(8,128)}, u32[]{:S(2)}) copy-start(f32[2048,204]{0,1:T(8,128)} %mul.212) | copy-start | bytes 5013508 | tf_op jit(solution)/shard_map/while
  66.3 3.9 %copy-start = (f32[2048,204]{0,1:T(8,128)S(1)}, f32[2048,204]{0,1:T(8,128)}, u32[]{:S(2)}) copy-start(f32[2048,204]{0,1:T(8,128)} %mul.212) | copy-start | bytes 5013508 | tf_op jit(solution)/shard_map/while
  73.6 3.9 %copy-start = (f32[2048,204]{0,1:T(8,128)S(1)}, f32[2048,204]{0,1:T(8,128)}, u32[]{:S(2)}) copy-start(f32[2048,204]{0,1:T(8,128)} %mul.212) | copy-start | bytes 5013508 | tf_op jit(solution)/shard_map/while
  80.8 3.9 %copy-start = (f32[2048,204]{0,1:T(8,128)S(1)}, f32[2048,204]{0,1:T(8,128)}, u32[]{:S(2)}) copy-start(f32[2048,204]{0,1:T(8,128)} %mul.212) | copy-start | bytes 5013508 | tf_op jit(solution)/shard_map/while
  88.0 3.9 %copy-start = (f32[2048,204]{0,1:T(8,128)S(1)}, f32[2048,204]{0,1:T(8,128)}, u32[]{:S(2)}) copy-start(f32[2048,204]{0,1:T(8,128)} %mul.212) | copy-start | bytes 5013508 | tf_op jit(solution)/shard_map/while
  95.3 3.9 %copy-start = (f32[2048,204]{0,1:T(8,128)S(1)}, f32[2048,204]{0,1:T(8,128)}, u32[]{:S(2)}) copy-start(f32[2048,204]{0,1:T(8,128)} %mul.212) | copy-start | bytes 5013508 | tf_op jit(solution)/shard_map/while
  102.5 3.9 %copy-start = (f32[2048,204]{0,1:T(8,128)S(1)}, f32[2048,204]{0,1:T(8,128)}, u32[]{:S(2)}) copy-start(f32[2048,204]{0,1:T(8,128)} %mul.212) | copy-start | bytes 5013508 | tf_op jit(solution)/shard_map/while
  109.8 3.9 %copy-start = (f32[2048,204]{0,1:T(8,128)S(1)}, f32[2048,204]{0,1:T(8,128)}, u32[]{:S(2)}) copy-start(f32[2048,204]{0,1:T(8,128)} %mul.212) | copy-start | bytes 5013508 | tf_op jit(solution)/shard_map/while
  117.0 3.9 %copy-start = (f32[2048,204]{0,1:T(8,128)S(1)}, f32[2048,204]{0,1:T(8,128)}, u32[]{:S(2)}) copy-start(f32[2048,204]{0,1:T(8,128)} %mul.212) | copy-start | bytes 5013508 | tf_op jit(solution)/shard_map/while
  124.3 3.9 %copy-start = (f32[2048,204]{0,1:T(8,128)S(1)}, f32[2048,204]{0,1:T(8,128)}, u32[]{:S(2)}) copy-start(f32[2048,204]{0,1:T(8,128)} %mul.212) | copy-start | bytes 5013508 | tf_op jit(solution)/shard_map/while
  131.5 3.9 %copy-start = (f32[2048,204]{0,1:T(8,128)S(1)}, f32[2048,204]{0,1:T(8,128)}, u32[]{:S(2)}) copy-start(f32[2048,204]{0,1:T(8,128)} %mul.212) | copy-start | bytes 5013508 | tf_op jit(solution)/shard_map/while
  138.7 3.9 %copy-start = (f32[2048,204]{0,1:T(8,128)S(1)}, f32[2048,204]{0,1:T(8,128)}, u32[]{:S(2)}) copy-start(f32[2048,204]{0,1:T(8,128)} %mul.212) | copy-start | bytes 5013508 | tf_op jit(solution)/shard_map/while
  144.1 11.1 %copy-start.1 = (bf16[40,6,2,16,128]{4,3,2,1,0:T(8,128)(2,1)S(1)}, bf16[40,6,2,16,128]{4,3,2,1,0:T(8,128)(2,1)}, u32[]{:S(2)}) copy-start(bf16[40,6,2,16,128]{4,3,2,1,0:T(8,128)(2,1)} %param.23) | copy-start | bytes 5898244
  144.2 4.0 %collective-permute-start = (f32[12,17]{1,0:T(8,128)S(1)}, f32[12,17]{1,0:T(8,128)S(1)}, u32[]{:S(2)}, u32[]{:S(2)}) collective-permute-start(f32[12,17]{1,0:T(8,128)S(1)} %reshape.292), channel_id=1, source_target_pairs={{0,2},{1,3},{4,6},{5,7},{8,10},{9,11},{12,14},{13,15},{16,18},{17,... | collective-permute-start | bytes 2456 | tf_op jit(solution)/shard_map/ppermute | solution.py:11
  148.9 4.1 %collective-permute-start.1 = (f32[12,128]{1,0:T(8,128)S(1)}, f32[12,128]{1,0:T(8,128)S(1)}, u32[]{:S(2)}, u32[]{:S(2)}) collective-permute-start(f32[12,128]{1,0:T(8,128)S(1)} %scatter-add.11), channel_id=1, source_target_pairs={{0,4},{4,8},{8,12},{12,16},{16,20},{20,24},{24,28},{1,5},{5,9},{9,... | collective-permute-start | bytes 18440 | tf_op jit(solution)/shard_map/ppermute | solution.py:11
  155.8 5.9 %collective-permute-start.2 = (f32[40,2,1,128]{3,0,2,1:T(8,128)S(1)}, f32[40,2,1,128]{3,0,2,1:T(8,128)S(1)}, u32[]{:S(2)}, u32[]{:S(2)}) collective-permute-start(f32[40,2,1,128]{3,0,2,1:T(8,128)S(1)} %copy.66), channel_id=1, source_target_pairs={{0,4},{4,8},{8,12},{12,16},{16,20},{20,24},{24,28},{1,5},{5,9},{9,... | collective-permute-start | bytes 122888 | tf_op jit(solution)/shard_map/ppermute | solution.py:21
  160.0 6.5 %collective-permute-start.3 = (f32[40,2,1,128]{3,0,2,1:T(8,128)S(1)}, f32[40,2,1,128]{3,0,2,1:T(8,128)S(1)}, u32[]{:S(2)}, u32[]{:S(2)}) collective-permute-start(f32[40,2,1,128]{3,0,2,1:T(8,128)S(1)} %copy.67), channel_id=1, source_target_pairs={{4,0},{8,4},{12,8},{16,12},{20,16},{24,20},{28,24},{5,1},{9,5},{13... | collective-permute-start | bytes 122888 | tf_op jit(solution)/shard_map/ppermute | solution.py:22
  167.5 6.2 %collective-permute-start.4 = (f32[40,2,18,1]{0,2,3,1:T(8,128)S(1)}, f32[40,2,18,1]{0,2,3,1:T(8,128)S(1)}, u32[]{:S(2)}, u32[]{:S(2)}) collective-permute-start(f32[40,2,18,1]{0,2,3,1:T(8,128)S(1)} %copy.70), channel_id=1, source_target_pairs={{0,2},{1,3},{4,6},{5,7},{8,10},{9,11},{12,14},{13,15},{16,18},{17,... | collective-permute-start | bytes 17288 | tf_op jit(solution)/shard_map/ppermute | solution.py:21
  172.1 5.7 %collective-permute-start.5 = (f32[40,2,18,1]{0,2,3,1:T(8,128)S(1)}, f32[40,2,18,1]{0,2,3,1:T(8,128)S(1)}, u32[]{:S(2)}, u32[]{:S(2)}) collective-permute-start(f32[40,2,18,1]{0,2,3,1:T(8,128)S(1)} %copy.71), channel_id=1, source_target_pairs={{2,0},{3,1},{6,4},{7,5},{10,8},{11,9},{14,12},{15,13},{18,16},{19,... | collective-permute-start | bytes 17288 | tf_op jit(solution)/shard_map/ppermute | solution.py:22
